TPU v7x, 32 devices: a whole 2x2x4 slice. The times are simulated.
32 devices in a mesh: section: 4 (over y, x), dp: 8 (over z, core).
Axes of the slice: x: 2, y: 2, z: 4, core: 2. Of those that a mesh axis runs over, the one named last changes fastest.
Arguments:
- inputs: bfloat16 [4, 2, 512, 4096], P('section', None, 'dp'), may hold values from -6 to 6
- cotangent: bfloat16 [2, 512, 4096], P(None, 'dp'), may hold values from -6 to 6
- norm_gain: bfloat16 [4, 4096], P('section', 'dp'), may hold values from 0.5 to 1.5
- key_weight: bfloat16 [4, 4096, 512], P('section', 'dp'), may hold values from -0.09375 to 0.09375
- value_weight: bfloat16 [4, 4096, 512], P('section', 'dp'), may hold values from -0.09375 to 0.09375
- plan: int32 [4, 2], P('section'), may hold values from 0 to 1, each once within a row
Outputs:
- grad_inputs: bfloat16 [4, 2, 512, 4096], P('section', None, 'dp')
- key_weight_grad: float32 [4, 4096, 512], P('section', 'dp')
- value_weight_grad: float32 [4, 4096, 512], P('section', 'dp')
- gain_grad: float32 [4, 4096], P('section', 'dp')
Inputs may be any that keep to these rules, and one draw needn't show every extreme that they name: Each row of plan lists every micro-batch once.
All inputs are finite; a program needn't handle non-finite values.
Results may differ from a plain program's by a relative error of at most 0.03.
Values may be sent and summed in bfloat16 or wider, within the bound.
A program may use at most 128 MiB of HBM per device.

v0:
```python
import math

import jax
import jax.numpy as jnp
from jax import lax
from jax.sharding import PartitionSpec as P

HEADS = 32
KV_HEADS = 4
HEAD_DIM = 128
GROUP = 8


eps = 1e-05
rope_base = 500000.0


def from_behind(value, axis, steps):
    count = lax.axis_size(axis)
    first, last = (max(0, -steps), min(count, count - steps))
    return lax.ppermute(value, axis, [(source, source + steps) for source in range(first, last)])


def rope_tables(length, head_dim):
    half_dim = head_dim // 2
    frequency = rope_base ** (-(jnp.arange(half_dim, dtype=jnp.float32) * 2.0 / head_dim))
    angles = jnp.arange(length, dtype=jnp.float32)[:, None] * frequency[None, :]
    cosine = jnp.concatenate([jnp.cos(angles), jnp.cos(angles)], axis=-1)
    sine_tab = jnp.concatenate([jnp.sin(angles), jnp.sin(angles)], axis=-1)
    return (cosine[:, None, :], sine_tab[:, None, :])


def turned(values):
    half_dim = values.shape[-1] // 2
    return jnp.concatenate([-values[..., half_dim:], values[..., :half_dim]], axis=-1)


def rotate(values, cosine, sine_tab):
    return values * cosine + turned(values) * sine_tab


def unrotate(values, cosine, sine_tab):
    return values * cosine - turned(values) * sine_tab


def contract_rows(left, right):
    return lax.dot_general(
        left, right, (((0,), (0,)), ((), ())), preferred_element_type=jnp.float32
    )


def contract_cols(left, right):
    return lax.dot_general(
        left, right, (((1,), (1,)), ((), ())), preferred_element_type=jnp.float32
    )


def body(inputs, cotangent, norm_gain, key_weight, value_weight, plan):
    sections = lax.axis_size("section")
    section_index = lax.axis_index("section")
    batches = inputs.shape[1]
    local_tok = inputs.shape[2]
    model_width = inputs.shape[3]
    kv_width = key_weight.shape[2]
    head_dim = HEAD_DIM
    key_heads = KV_HEADS
    query_heads = HEADS
    group_count = GROUP
    score_scale = 1.0 / math.sqrt(head_dim)
    all_rows = batches * local_tok
    widened = inputs[0].reshape(all_rows, model_width).astype(jnp.float32)
    inv_rms = lax.rsqrt(jnp.mean(widened * widened, axis=-1, keepdims=True) + eps)
    full_key, full_value, full_gain = (
        lax.all_gather(key_weight[0], "dp", axis=0, tiled=True),
        lax.all_gather(value_weight[0], "dp", axis=0, tiled=True),
        lax.all_gather(norm_gain[0], "dp", axis=0, tiled=True),
    )
    gain_full = full_gain.astype(jnp.float32)
    normed = (widened * inv_rms * gain_full).astype(jnp.bfloat16)
    key_pre = jnp.dot(normed, full_key, preferred_element_type=jnp.float32)
    value_pre = jnp.dot(normed, full_value, preferred_element_type=jnp.float32)
    cosine, sine_tab = rope_tables(local_tok, head_dim)
    key_rot = rotate(
        key_pre.reshape(batches, local_tok, key_heads, head_dim), cosine, sine_tab
    ).astype(jnp.bfloat16)
    value_heads = value_pre.astype(jnp.bfloat16).reshape(batches, local_tok, key_heads, head_dim)
    query_rot = rotate(
        normed.astype(jnp.float32).reshape(batches, local_tok, query_heads, head_dim),
        cosine,
        sine_tab,
    ).astype(jnp.bfloat16)
    query_rot = query_rot.reshape(batches, local_tok, key_heads, group_count, head_dim)
    scores = (
        jnp.einsum("blkgd,bmkd->bkglm", query_rot, key_rot, preferred_element_type=jnp.float32)
        * score_scale
    )
    causal = jnp.arange(local_tok)[:, None] >= jnp.arange(local_tok)[None, :]
    raised = jnp.where(causal, jnp.exp(scores), 0.0)
    attn_prob = raised / jnp.sum(raised, axis=-1, keepdims=True)
    prob_low = attn_prob.astype(jnp.bfloat16)

    def busy_turn(operands):
        slot_index, incoming, stores = operands
        lower_store, key_store, value_store, sum_gain, sum_key, sum_value = stores
        first_row = slot_index * local_tok
        own_cotangent = lax.dynamic_index_in_dim(cotangent, slot_index, 0, keepdims=False)
        upper_grad = jnp.where(section_index == sections - 1, own_cotangent, incoming)
        part_wide = lax.dynamic_slice_in_dim(widened, first_row, local_tok, 0)
        part_inv = lax.dynamic_slice_in_dim(inv_rms, first_row, local_tok, 0)
        part_query = lax.dynamic_index_in_dim(query_rot, slot_index, 0, keepdims=False)
        part_key = lax.dynamic_index_in_dim(key_rot, slot_index, 0, keepdims=False)
        part_value = lax.dynamic_index_in_dim(value_heads, slot_index, 0, keepdims=False)
        part_prob = lax.dynamic_index_in_dim(attn_prob, slot_index, 0, keepdims=False)
        part_low = lax.dynamic_index_in_dim(prob_low, slot_index, 0, keepdims=False)
        grad_heads = upper_grad.reshape(local_tok, key_heads, group_count, head_dim)
        grad_prob = jnp.einsum(
            "lkgd,mkd->kglm", grad_heads, part_value, preferred_element_type=jnp.float32
        )
        grad_value = jnp.einsum(
            "kglm,lkgd->mkd", part_low, grad_heads, preferred_element_type=jnp.float32
        ).astype(jnp.bfloat16)
        row_dot = jnp.sum(part_prob * grad_prob, axis=-1, keepdims=True)
        grad_score = (part_prob * (grad_prob - row_dot) * score_scale).astype(jnp.bfloat16)
        grad_query = jnp.einsum(
            "kglm,mkd->lkgd", grad_score, part_key, preferred_element_type=jnp.float32
        )
        grad_key = jnp.einsum(
            "kglm,lkgd->mkd", grad_score, part_query, preferred_element_type=jnp.float32
        )
        query_back = unrotate(
            grad_query.reshape(local_tok, query_heads, head_dim), cosine, sine_tab
        ).reshape(local_tok, model_width)
        key_back = (
            unrotate(grad_key, cosine, sine_tab).astype(jnp.bfloat16).reshape(local_tok, kv_width)
        )
        value_flat = grad_value.reshape(local_tok, kv_width)
        grad_normed = query_back + (
            contract_cols(key_back, full_key) + contract_cols(value_flat, full_value)
        )
        gain_term = grad_normed * part_wide * part_inv
        projected = jnp.mean(gain_term * gain_full, axis=-1, keepdims=True)
        lower_grad = (
            upper_grad.astype(jnp.float32)
            + part_inv * gain_full * grad_normed
            - part_wide * part_inv * part_inv * projected
        )
        lower_grad = lower_grad.astype(jnp.bfloat16)
        lower_store = lax.dynamic_update_index_in_dim(lower_store, lower_grad, slot_index, 0)
        key_store = lax.dynamic_update_slice_in_dim(key_store, key_back, first_row, 0)
        value_store = lax.dynamic_update_slice_in_dim(value_store, value_flat, first_row, 0)
        sum_gain = sum_gain + jnp.sum(gain_term, axis=0)
        return (lower_grad, (lower_store, key_store, value_store, sum_gain, sum_key, sum_value))

    def quiet_turn(operands):
        return (jnp.zeros((local_tok, model_width), jnp.bfloat16), operands[2])

    def one_turn(turn_index, carried):
        incoming, stores = carried
        slot_index = turn_index - (sections - 1 - section_index)
        active = (slot_index >= 0) & (slot_index < batches)
        clipped = jnp.clip(slot_index, 0, batches - 1)
        lower_grad, stores = lax.cond(active, busy_turn, quiet_turn, (clipped, incoming, stores))
        incoming = from_behind(lower_grad, "section", -1)
        return (incoming, stores)

    stores = (
        jnp.zeros((batches, local_tok, model_width), jnp.bfloat16),
        jnp.zeros((all_rows, kv_width), jnp.bfloat16),
        jnp.zeros((all_rows, kv_width), jnp.bfloat16),
        jnp.zeros((model_width,), jnp.float32),
        jnp.zeros((model_width, kv_width), jnp.float32),
        jnp.zeros((model_width, kv_width), jnp.float32),
    )
    incoming = jnp.zeros((local_tok, model_width), jnp.bfloat16)
    incoming, stores = lax.fori_loop(0, sections - 1 + batches, one_turn, (incoming, stores))
    lower_store, key_store, value_store, sum_gain, sum_key, sum_value = stores
    sum_key = contract_rows(normed, key_store)
    sum_value = contract_rows(normed, value_store)
    summed = (
        lax.psum_scatter(
            sum_key.astype(jnp.bfloat16), "dp", scatter_dimension=0, tiled=True
        ).astype(jnp.float32),
        lax.psum_scatter(
            sum_value.astype(jnp.bfloat16), "dp", scatter_dimension=0, tiled=True
        ).astype(jnp.float32),
        lax.psum_scatter(
            sum_gain.astype(jnp.bfloat16), "dp", scatter_dimension=0, tiled=True
        ).astype(jnp.float32),
    )
    selector = plan[0][:, None] == jnp.arange(batches, dtype=jnp.int32)[None, :]
    ordered = jnp.sum(
        jnp.where(selector[:, :, None, None], lower_store[None], jnp.zeros((), jnp.bfloat16)),
        axis=1,
    )
    return (ordered[None], summed[0][None], summed[1][None], summed[2][None])


def solution(mesh):
    in_specs = (
        P("section", None, "dp", None),
        P(None, "dp", None),
        P("section", "dp"),
        P("section", "dp", None),
        P("section", "dp", None),
        P("section", None),
    )
    out_specs = (
        P("section", None, "dp", None),
        P("section", "dp", None),
        P("section", "dp", None),
        P("section", "dp"),
    )
    return jax.shard_map(body, mesh=mesh, in_specs=in_specs, out_specs=out_specs, check_vma=False)
```

profile of v0, /device:TPU:0, one launch (start us, length us, event | category | flops | bytes accessed | tf_op | source)
XLA Modules:
  0.0 428.3 jit_solution(13967941510831594862)
XLA Ops:
  8.7 1.4 convert_element_type.109
  11.4 14.6 %all-gather = bf16[1,4096]{1,0:T(2,128)(2,1)S(1)} all-gather(bf16[1,512]{1,0:T(2,128)(2,1)S(1)} %copy-done.20), channel_id=2, replica_groups=mesh['section'=4,'dp'=8] {'dp'}, dimensions={1}, use_global_device_ids=true | all-gather | bytes 9216 | tf_op jit(solution)/shard_map/all_gather | solution.py:76
  30.3 1.4 copy.46
  32.0 27.2 %all-gather.6.cloned.1.call-done = bf16[1,4096,512]{2,1,0:T(8,128)(2,1)} async-done(((bf16[1,512,512]{2,1,0:T(8,128)(2,1)}), bf16[1,4096,512]{2,1,0:T(8,128)(2,1)}) %all-gather.6.cloned.1.call-update) | async-done | bytes 4194320 | tf_op jit(solution)/shard_map/all_gather | solution.py:74
  59.2 6.5 %copy.45 = bf16[512,4096]{1,0:T(8,128)(2,1)} copy(bf16[512,4096]{0,1:T(8,128)(2,1)} %bitcast.220) | data formatting | bytes 8388608 | tf_op jit(solution)/shard_map/dot_general | solution.py:80
  65.7 4.0 fusion.56
  70.6 3.6 fusion.140
  74.2 3.3 copy.49
  77.5 29.0 %all-gather.8.cloned.1.call-done = bf16[1,4096,512]{2,1,0:T(8,128)(2,1)} async-done(((bf16[1,512,512]{2,1,0:T(8,128)(2,1)}), bf16[1,4096,512]{2,1,0:T(8,128)(2,1)}) %all-gather.8.cloned.1.call-update) | async-done | bytes 4194320 | tf_op jit(solution)/shard_map/all_gather | solution.py:75
  106.5 2.9 convolution_convert_fusion.2
  113.2 204.3 %while.22 = (s32[]{:T(128)}, bf16[64,4096]{1,0:T(8,128)(2,1)S(1)}, bf16[2,64,4096]{2,1,0:T(8,128)(2,1)}, bf16[128,512]{1,0:T(8,128)(2,1)}, bf16[128,512]{1,0:T(8...) while((s32[]{:T(128)}, bf16[64,4096]{1,0:T(8,128)(2,1)S(1)}, ...), condition=%wide.region_8.9_spmd, body=%wide.region_2.8_spmd.sunk | while | flops 678678656 | bytes 91856312 | solution.py:175
  114.0 1.3 collective-permute-start
  115.3 14.9 %collective-permute-done = bf16[64,4096]{1,0:T(8,128)(2,1)S(1)} collective-permute-done((bf16[64,4096]{1,0:T(8,128)(2,1)}, bf16[64,4096]{1,0:T(8,128)(2,1)S(1)}, u32[]{:S(2)}, u32[]{:S(2)}) %collective-permute-start) | collective-permute-done | bytes 524320 | tf_op jit(solution)/shard_map/while/body/eval_jaxpr/ppermute | solution.py:21
  131.0 1.3 collective-permute-start
  132.3 14.6 %collective-permute-done = bf16[64,4096]{1,0:T(8,128)(2,1)S(1)} collective-permute-done((bf16[64,4096]{1,0:T(8,128)(2,1)}, bf16[64,4096]{1,0:T(8,128)(2,1)S(1)}, u32[]{:S(2)}, u32[]{:S(2)}) %collective-permute-start) | collective-permute-done | bytes 524320 | tf_op jit(solution)/shard_map/while/body/eval_jaxpr/ppermute | solution.py:21
  149.1 87.7 %collective-permute-done = bf16[64,4096]{1,0:T(8,128)(2,1)S(1)} collective-permute-done((bf16[64,4096]{1,0:T(8,128)(2,1)}, bf16[64,4096]{1,0:T(8,128)(2,1)S(1)}, u32[]{:S(2)}, u32[]{:S(2)}) %collective-permute-start) | collective-permute-done | bytes 524320 | tf_op jit(solution)/shard_map/while/body/eval_jaxpr/ppermute | solution.py:21
  236.8 26.1 %conditional.2 = (bf16[64,4096]{1,0:T(8,128)(2,1)}, bf16[2,64,4096]{2,1,0:T(8,128)(2,1)}, bf16[128,512]{1,0:T(8,128)(2,1)}, bf16[128,512]{1,0:T(8,128)(2,1)}, f32[4096]{0:T(1024)}) conditional(s32[]{:T(128)} %convert_element_type.179, (bf16[2,64,4096]{2,1,0:T(8,128)(2,1)}, bf16[128,512]{1,0:T(8,128)(2,1)}, bf16[128,512]{1,0:T(8,128)(2,1)}, ...), branch_computations={%region_3.3_spmd, %region_4.7_spmd} | conditional | flops 678678656 | bytes 89758680 | solution.py:162
  236.8 1.3 fusion.23
  238.9 2.4 convolution_bitcast_fusion
  241.4 2.1 convolution_bitcast_fusion.1
  243.6 4.6 %fusion.29 = f32[64,4096]{1,0:T(8,128)} fusion(bf16[4096,512]{1,0:T(8,128)(2,1)} %get-tuple-element.461, f32[64,4,64]{2,0,1:T(8,128)S(1)} %get-tuple-element.641, f32[64,4,64]{2,0,1:T(8,128)S(1)} %get-tuple-element.640, f32[64,4,128]{2,0,1:T(8,128)S(1)} %convolution_bitcast_fusion.1, f32[64,128]{1,0:T(8,128)} %bitcast.14, f32[64,128]{1,0:T(8,128)} %bitcast.11), kind=kOutput, calls=%fused_computation.44 | convolution fusion | flops 268599296 | bytes 5570560 | tf_op jit(solution)/shard_map/while/body/eval_jaxpr/cond/branch_1_fun/dot_general | solution.py:53
  249.5 2.0 fusion.11
  252.6 1.9 fusion.7
  255.3 3.4 fusion.26
  260.0 1.3 add.76
  261.3 1.5 bitcast_dynamic-update-slice_fusion.1
  262.8 1.3 collective-permute-start
  264.1 13.7 %collective-permute-done = bf16[64,4096]{1,0:T(8,128)(2,1)S(1)} collective-permute-done((bf16[64,4096]{1,0:T(8,128)(2,1)}, bf16[64,4096]{1,0:T(8,128)(2,1)S(1)}, u32[]{:S(2)}, u32[]{:S(2)}) %collective-permute-start) | collective-permute-done | bytes 524320 | tf_op jit(solution)/shard_map/while/body/eval_jaxpr/ppermute | solution.py:21
  277.9 26.1 %conditional.2 = (bf16[64,4096]{1,0:T(8,128)(2,1)}, bf16[2,64,4096]{2,1,0:T(8,128)(2,1)}, bf16[128,512]{1,0:T(8,128)(2,1)}, bf16[128,512]{1,0:T(8,128)(2,1)}, f32[4096]{0:T(1024)}) conditional(s32[]{:T(128)} %convert_element_type.179, (bf16[2,64,4096]{2,1,0:T(8,128)(2,1)}, bf16[128,512]{1,0:T(8,128)(2,1)}, bf16[128,512]{1,0:T(8,128)(2,1)}, ...), branch_computations={%region_3.3_spmd, %region_4.7_spmd} | conditional | flops 678678656 | bytes 89758680 | solution.py:162
  277.9 1.3 fusion.23
  280.0 2.4 convolution_bitcast_fusion
  282.5 2.1 convolution_bitcast_fusion.1
  284.7 4.6 %fusion.29 = f32[64,4096]{1,0:T(8,128)} fusion(bf16[4096,512]{1,0:T(8,128)(2,1)} %get-tuple-element.461, f32[64,4,64]{2,0,1:T(8,128)S(1)} %get-tuple-element.641, f32[64,4,64]{2,0,1:T(8,128)S(1)} %get-tuple-element.640, f32[64,4,128]{2,0,1:T(8,128)S(1)} %convolution_bitcast_fusion.1, f32[64,128]{1,0:T(8,128)} %bitcast.14, f32[64,128]{1,0:T(8,128)} %bitcast.11), kind=kOutput, calls=%fused_computation.44 | convolution fusion | flops 268599296 | bytes 5570560 | tf_op jit(solution)/shard_map/while/body/eval_jaxpr/cond/branch_1_fun/dot_general | solution.py:53
  290.6 2.0 fusion.11
  293.6 1.9 fusion.7
  296.4 3.4 fusion.26
  301.1 1.3 add.76
  302.4 1.5 bitcast_dynamic-update-slice_fusion.1
  303.9 1.3 collective-permute-start
  305.2 12.3 %collective-permute-done = bf16[64,4096]{1,0:T(8,128)(2,1)S(1)} collective-permute-done((bf16[64,4096]{1,0:T(8,128)(2,1)}, bf16[64,4096]{1,0:T(8,128)(2,1)S(1)}, u32[]{:S(2)}, u32[]{:S(2)}) %collective-permute-start) | collective-permute-done | bytes 524320 | tf_op jit(solution)/shard_map/while/body/eval_jaxpr/ppermute | solution.py:21
  317.5 4.5 %convolution_convert_fusion = bf16[4096,512]{1,0:T(8,128)(2,1)} fusion(bf16[128,4096]{1,0:T(8,128)(2,1)} %copy-done.8, bf16[128,512]{1,0:T(8,128)(2,1)} %get-tuple-element.506), kind=kOutput, calls=%fused_computation.63 | convolution fusion | flops 538968064 | bytes 5373952 | tf_op jit(solution)/shard_map/dot_general | solution.py:47
  323.2 4.2 convolution_convert_fusion.1
  330.0 14.9 %all-reduce = bf16[4096]{0:T(1024)(128)(2,1)S(1)} all-reduce(bf16[4096]{0:T(1024)(128)(2,1)S(1)} %convert_element_type.130), channel_id=7, replica_groups=mesh['section'=4,'dp'=8] {'dp'}, use_global_device_ids=true, to_apply=%region_12.13.clone | all-reduce | flops 4096 | bytes 16384
  345.6 1.6 select_reduce_fusion
  347.2 22.5 %reduce-scatter.5.cloned.1.call-done = bf16[512,512]{1,0:T(8,128)(2,1)} async-done(((bf16[4096,512]{1,0:T(8,128)(2,1)}), bf16[512,512]{1,0:T(8,128)(2,1)}) %reduce-scatter.5.cloned.1.call-update) | async-done | bytes 524304 | tf_op jit(solution)/shard_map/reduce_scatter | solution.py:183
  369.6 2.1 bitcast_convert_fusion
  371.8 47.8 %reduce-scatter.3.cloned.1.call-done = bf16[512,512]{1,0:T(8,128)(2,1)} async-done(((bf16[4096,512]{1,0:T(8,128)(2,1)}), bf16[512,512]{1,0:T(8,128)(2,1)}) %reduce-scatter.3.cloned.1.call-update) | async-done | bytes 524304 | tf_op jit(solution)/shard_map/reduce_scatter | solution.py:180
  419.6 2.1 bitcast_convert_fusion.1
  (126 shorter events, 32.8 us)
Async XLA Ops:
  7.2 3.0 copy-start.11
  7.2 52.1 %all-gather.6.cloned.1.call-start = ((), (), s32[]{:S(2)}) async-start(), calls=%async_computation.4 | async-start | bytes 4718592 | tf_op jit(solution)/shard_map/all_gather | solution.py:74
  7.9 98.6 %all-gather.8.cloned.1.call-start = ((), (), s32[]{:S(2)}) async-start(), calls=%async_computation.5 | async-start | bytes 4718592 | tf_op jit(solution)/shard_map/all_gather | solution.py:75
  8.7 2.8 copy-start.20
  8.7 361.0 %reduce-scatter.5.cloned.1.call-start = ((), (), s32[]{:S(2)}) async-start(), calls=%async_computation.3 | async-start | bytes 4718592 | tf_op jit(solution)/shard_map/reduce_scatter | solution.py:183
  10.2 16.3 %copy-start.4 = (f32[1,2,64,4096]{3,2,1,0:T(8,128)}, f32[1,2,64,4096]{3,2,1,0:T(8,128)S(1)}, u32[]{:S(2)}) copy-start(f32[1,2,64,4096]{3,2,1,0:T(8,128)S(1)} %convert_element_type.109) | copy-start | bytes 6291460
  10.5 17.9 %copy-start.18 = (f32[2,64]{1,0:T(2,128)}, f32[2,64]{1,0:T(2,128)S(1)}, u32[]{:S(2)}) copy-start(f32[2,64]{1,0:T(2,128)S(1)} %add_rsqrt_fusion) | copy-start | bytes 1540
  29.3 1.0 copy-start.16
  30.3 1.4 copy-start.12
  32.0 74.5 %copy-start.8 = (bf16[128,4096]{1,0:T(8,128)(2,1)}, bf16[128,4096]{1,0:T(8,128)(2,1)S(1)}, u32[]{:S(2)}) copy-start(bf16[128,4096]{1,0:T(8,128)(2,1)S(1)} %multiply_convert_fusion) | copy-start | bytes 3145732
  59.2 6.5 %copy-start.19 = (f32[2,64]{1,0:T(2,128)S(1)}, f32[2,64]{1,0:T(2,128)}, u32[]{:S(2)}) copy-start(f32[2,64]{1,0:T(2,128)} %copy-done.18) | copy-start | bytes 1540
  114.0 16.2 %collective-permute-start = (bf16[64,4096]{1,0:T(8,128)(2,1)}, bf16[64,4096]{1,0:T(8,128)(2,1)S(1)}, u32[]{:S(2)}, u32[]{:S(2)}) collective-permute-start(bf16[64,4096]{1,0:T(8,128)(2,1)} %get-tuple-element.791), channel_id=1, source_target_pairs={{8,0},{16,8},{24,16},{9,1},{17,9},{25,17},{10,2},{18,10},{26,18},{... | collective-permute-start | bytes 1572872 | tf_op jit(solution)/shard_map/while/body/eval_jaxpr/ppermute | solution.py:21
  131.0 15.9 %collective-permute-start = (bf16[64,4096]{1,0:T(8,128)(2,1)}, bf16[64,4096]{1,0:T(8,128)(2,1)S(1)}, u32[]{:S(2)}, u32[]{:S(2)}) collective-permute-start(bf16[64,4096]{1,0:T(8,128)(2,1)} %get-tuple-element.791), channel_id=1, source_target_pairs={{8,0},{16,8},{24,16},{9,1},{17,9},{25,17},{10,2},{18,10},{26,18},{... | collective-permute-start | bytes 1572872 | tf_op jit(solution)/shard_map/while/body/eval_jaxpr/ppermute | solution.py:21
  147.8 89.0 %collective-permute-start = (bf16[64,4096]{1,0:T(8,128)(2,1)}, bf16[64,4096]{1,0:T(8,128)(2,1)S(1)}, u32[]{:S(2)}, u32[]{:S(2)}) collective-permute-start(bf16[64,4096]{1,0:T(8,128)(2,1)} %get-tuple-element.791), channel_id=1, source_target_pairs={{8,0},{16,8},{24,16},{9,1},{17,9},{25,17},{10,2},{18,10},{26,18},{... | collective-permute-start | bytes 1572872 | tf_op jit(solution)/shard_map/while/body/eval_jaxpr/ppermute | solution.py:21
  236.8 4.6 %copy-start.6 = (bf16[64,4096]{1,0:T(8,128)(2,1)}, bf16[64,4096]{1,0:T(8,128)(2,1)S(1)}, u32[]{:S(2)}) copy-start(bf16[64,4096]{1,0:T(8,128)(2,1)S(1)} %get-tuple-element.452) | copy-start | bytes 1572868 | tf_op jit(solution)/shard_map/while/body/eval_jaxpr/cond
  238.1 0.8 copy-start.1
  251.5 1.1 copy-start.2
  251.5 3.8 copy-start.3
  251.5 3.8 copy-start.5
  251.9 3.4 copy-start
  251.9 3.4 copy-start.17
  255.3 3.4 copy-start.7
  255.3 3.4 copy-start.10
  255.3 3.4 copy-start.13
  260.0 2.8 copy-start.14
  262.8 15.0 %collective-permute-start = (bf16[64,4096]{1,0:T(8,128)(2,1)}, bf16[64,4096]{1,0:T(8,128)(2,1)S(1)}, u32[]{:S(2)}, u32[]{:S(2)}) collective-permute-start(bf16[64,4096]{1,0:T(8,128)(2,1)} %get-tuple-element.791), channel_id=1, source_target_pairs={{8,0},{16,8},{24,16},{9,1},{17,9},{25,17},{10,2},{18,10},{26,18},{... | collective-permute-start | bytes 1572872 | tf_op jit(solution)/shard_map/while/body/eval_jaxpr/ppermute | solution.py:21
  277.9 4.6 %copy-start.6 = (bf16[64,4096]{1,0:T(8,128)(2,1)}, bf16[64,4096]{1,0:T(8,128)(2,1)S(1)}, u32[]{:S(2)}) copy-start(bf16[64,4096]{1,0:T(8,128)(2,1)S(1)} %get-tuple-element.452) | copy-start | bytes 1572868 | tf_op jit(solution)/shard_map/while/body/eval_jaxpr/cond
  279.2 0.8 copy-start.1
  292.6 1.1 copy-start.2
  292.6 3.8 copy-start.3
  292.6 3.8 copy-start.5
  293.0 3.4 copy-start
  293.0 3.4 copy-start.17
  296.4 3.4 copy-start.7
  296.4 3.4 copy-start.10
  296.4 3.4 copy-start.13
  301.1 2.8 copy-start.14
  303.9 13.6 %collective-permute-start = (bf16[64,4096]{1,0:T(8,128)(2,1)}, bf16[64,4096]{1,0:T(8,128)(2,1)S(1)}, u32[]{:S(2)}, u32[]{:S(2)}) collective-permute-start(bf16[64,4096]{1,0:T(8,128)(2,1)} %get-tuple-element.791), channel_id=1, source_target_pairs={{8,0},{16,8},{24,16},{9,1},{17,9},{25,17},{10,2},{18,10},{26,18},{... | collective-permute-start | bytes 1572872 | tf_op jit(solution)/shard_map/while/body/eval_jaxpr/ppermute | solution.py:21
  321.9 1.2 copy-start.9
  322.0 97.6 %reduce-scatter.3.cloned.1.call-start = ((), (), s32[]{:S(2)}) async-start(), calls=%async_computation.2 | async-start | bytes 4718592 | tf_op jit(solution)/shard_map/reduce_scatter | solution.py:180
  327.3 0.7 copy-start.22
  327.3 1.9 copy-start.21
  327.3 18.2 %copy-start.15 = (bf16[2,64,4096]{2,1,0:T(8,128)(2,1)S(1)}, bf16[2,64,4096]{2,1,0:T(8,128)(2,1)}, u32[]{:S(2)}) copy-start(bf16[2,64,4096]{2,1,0:T(8,128)(2,1)} %get-tuple-element.504) | copy-start | bytes 3145732
Sparse Core Ops, SparseCore 0:
  9.6 49.6 all-gather.5
  60.8 45.6 all-gather.7
  322.1 47.5 reduce-scatter.4
  371.8 47.7 reduce-scatter.2
where the time goes:
time: 430 us; the launch traced here: 428 us
  waiting for transfers between devices  271 us (63%)
  matrix products  51.9 us (12%)
  blocking collectives  29.5 us (7%)
  local copies, waits for them, and re-layouts  29.3 us (7%)
  other arithmetic  24.8 us (6%)
  between operations  14.6 us (3%)
  starting transfers between devices  6.56 us (2%)
    ppermute x5, waiting for transfers between devices, from_behind(): lax.ppermute(value, axis, [(source, source + steps) for source in range(f...  143 us
    reduce_scatter x1, waiting for transfers between devices, body(): lax.psum_scatter(sum_key.astype(jnp.bfloat16), 'dp', scatter_dimension=0,...  47.8 us
    all_gather x1, waiting for transfers between devices, body(): lax.all_gather(value_weight[0], 'dp', axis=0, tiled=True)  29 us
    all_gather x1, waiting for transfers between devices, body(): lax.all_gather(key_weight[0], 'dp', axis=0, tiled=True)  27.2 us
    reduce_scatter x1, waiting for transfers between devices, body(): lax.psum_scatter(sum_value.astype(jnp.bfloat16), 'dp', scatter_dimension=...  22.5 us
    dot_general x4, matrix products, contract_cols(): lax.dot_general(left, right, (((1,), (1,)), ((), ())), preferred_element_...  16 us
    unnamed x1, blocking collectives  14.9 us
    all_gather x1, blocking collectives, body(): lax.all_gather(norm_gain[0], 'dp', axis=0, tiled=True)  14.6 us
  transfers between devices with their start and end apart: 9, of which 9 were waited for; matrix products, arithmetic and copies ran while one was open for 8% of the time, Pallas kernels for 0%

commit v1 on v0

v1 whole, which is shorter than its diff:
```python
import functools
import math

import jax
import jax.numpy as jnp
import numpy as np
from jax import lax
from jax.experimental import pallas as pl
from jax.experimental.pallas import tpu as pltpu
from jax.sharding import PartitionSpec as P

HEAD_DIM = 128
EPS = 1e-05
ROPE_BASE = 500000.0
PIECES = 2
MESH = pl.DeviceIdType.MESH
F32 = jnp.float32
BF16 = jnp.bfloat16


def dot_nn(a, b):
    return lax.dot_general(a, b, (((1,), (0,)), ((), ())), preferred_element_type=F32)


def dot_nt(a, b):
    return lax.dot_general(a, b, (((1,), (1,)), ((), ())), preferred_element_type=F32)


def dot_tn(a, b):
    return lax.dot_general(a, b, (((0,), (0,)), ((), ())), preferred_element_type=F32)


def rope_tables(length):
    half = HEAD_DIM // 2
    freq = (ROPE_BASE ** (-(np.arange(half, dtype=np.float32) * 2.0 / HEAD_DIM))).astype(np.float32)
    angles = np.arange(length, dtype=np.float32)[:, None] * freq[None, :]
    cos, sin = np.cos(angles), np.sin(angles)
    return (
        np.concatenate([cos, cos], -1).astype(np.float32),
        np.concatenate([-sin, sin], -1).astype(np.float32),
    )


def kernel(S, N, x_ref, cot_ref, gain_ref, wk_ref, wv_ref, cos_ref, sin_ref,
           low_out, gk_out, gv_out, gg_out,
           wall, ns, nall, gall, inv_s, acc, key_s, val_s, qst, prob, ubuf, lowb, gnb,
           kball, gsh, gsall,
           loc, ws, wr, rls, rlr, gsem, nsem, ssem, us, ur, uloc, kbs, kbr, krs, krr):
    B, KH, L = ubuf.shape[0], ubuf.shape[1], ubuf.shape[2]
    CW = ubuf.shape[3]
    w = wall.shape[1]
    KV = KH * HEAD_DIM
    G = CW // HEAD_DIM
    D = x_ref.shape[1]
    C = N // 2
    scale = 1.0 / math.sqrt(HEAD_DIM)
    sec = lax.axis_index("section")
    me = lax.axis_index("dp")
    c = me // 2
    core = me % 2
    partner = c * 2 + (1 - core)
    hp = w // PIECES

    def remote(src, dst, send, recv, peer):
        return pltpu.make_async_remote_copy(
            src_ref=src, dst_ref=dst, send_sem=send, recv_sem=recv,
            device_id=(sec, peer), device_id_type=MESH)

    def wait_all(ref, sem):
        pltpu.make_async_copy(ref, ref, sem).wait()

    ck = pltpu.make_async_copy(wk_ref, wall.at[me, :, pl.ds(0, KV)], loc.at[0])
    cv = pltpu.make_async_copy(wv_ref, wall.at[me, :, pl.ds(KV, KV)], loc.at[1])
    ck.start()
    cv.start()

    barrier = pltpu.get_barrier_semaphore()
    for i in range(1, N):
        pl.semaphore_signal(barrier, inc=1, device_id=(sec, (me + i) % N), device_id_type=MESH)

    @pl.when(sec > 0)
    def _():
        pl.semaphore_signal(barrier, inc=1, device_id=(sec - 1, me), device_id_type=MESH)

    @pl.when(sec < S - 1)
    def _():
        pl.semaphore_signal(barrier, inc=1, device_id=(sec + 1, me), device_id_type=MESH)
    below = jnp.where(sec > 0, 1, 0)
    above = jnp.where(sec < S - 1, 1, 0)
    pl.semaphore_wait(barrier, N - 1 + below + above)

    gcopies = []
    for i in range(1, N):
        cp = remote(gain_ref, gall.at[me], gsem.at[0], gsem.at[1], (me + i) % N)
        cp.start()
        gcopies.append(cp)
    gall[me] = gain_ref[...]
    ck.wait()
    cv.wait()

    def piece(shard, p):
        return wall.at[shard, pl.ds(p * hp, hp)]

    def wcopy(way, t, p):
        chip = c - t if way == 0 else c + t
        peer = (c + 1 if way == 0 else c - 1) * 2 + core
        ref = piece(chip * 2 + core, p)
        return remote(ref, ref, ws.at[way, t, p], wr.at[way, t, p], peer)

    def wrecv(way, t, p):
        chip = c - 1 - t if way == 0 else c + 1 + t
        ref = piece(chip * 2 + core, p)
        return remote(ref, ref, ws.at[way, t, p], wr.at[way, t, p], partner)

    def relay(slot, chip, p, mine):
        ref = piece(chip * 2 + (core if mine else 1 - core), p)
        return remote(ref, ref, rls.at[slot, p], rlr.at[slot, p], partner)

    def can_send(way, t):
        return ((c - t >= 0) & (c + 1 < C)) if way == 0 else ((c + t < C) & (c >= 1))

    def can_recv(way, t):
        return (c - 1 - t >= 0) if way == 0 else (c + 1 + t < C)

    for p in range(PIECES):
        for way in range(2):
            @pl.when(can_send(way, 0))
            def _(way=way, p=p):
                wcopy(way, 0, p).start()
        relay(0, c, p, True).start()

    def cot_copy(k, j):
        return pltpu.make_async_copy(
            cot_ref.at[k, :, pl.ds(j * CW, CW)], ubuf.at[k, j], uloc.at[k, j])

    @pl.when(sec == S - 1)
    def _():
        for k in range(B):
            for j in range(KH):
                cot_copy(k, j).start()

    total = jnp.zeros((B * L, 1), F32)
    for d in range(N):
        xd = x_ref[:, d * w:(d + 1) * w].astype(F32)
        total = total + jnp.sum(xd * xd, axis=-1, keepdims=True)
    inv = lax.rsqrt(total * (1.0 / D) + EPS)
    inv_s[...] = jnp.broadcast_to(inv, inv_s.shape)
    wait_all(gall.at[pl.ds(0, N - 1)], gsem.at[1])
    for d in range(N):
        xd = x_ref[:, d * w:(d + 1) * w].astype(F32)
        ns[d] = (xd * inv * gall[d][0:1, :]).astype(BF16)
        gsh[d] = jnp.zeros(gsh.shape[1:], F32)
    nall[me] = ns[me]
    cos = cos_ref[...]
    sin = sin_ref[...]

    def queries(k, carry):
        rows = pl.ds(pl.multiple_of(k * L, L), L)
        for j in range(KH):
            for g in range(G):
                col = (j * G + g) * HEAD_DIM
                v = ns[col // w, rows, col % w:col % w + HEAD_DIM].astype(F32)
                q = v * cos + pltpu.roll(v, HEAD_DIM // 2, 1) * sin
                qst[k, j, g * L:(g + 1) * L, :] = q.astype(BF16)
        return carry
    lax.fori_loop(0, B, queries, 0)

    def forward_step(t):
        for p in range(PIECES):
            for way in range(2):
                @pl.when(can_recv(way, t))
                def _(way=way, p=p):
                    wrecv(way, t, p).wait_recv()
                    if t + 1 < C - 1:
                        @pl.when(can_send(way, t + 1))
                        def _():
                            wcopy(way, t + 1, p).start()
                    chip = c - 1 - t if way == 0 else c + 1 + t
                    relay(1 + way * (C - 1) + t, chip, p, True).start()

    def use_step(t):
        for way in range(2):
            @pl.when(can_recv(way, t))
            def _(way=way):
                chip = c - 1 - t if way == 0 else c + 1 + t
                for p in range(PIECES):
                    relay(1 + way * (C - 1) + t, chip, p, False).wait_recv()
                acc[...] += dot_nn(ns[chip * 2], wall[chip * 2]) + dot_nn(
                    ns[chip * 2 + 1], wall[chip * 2 + 1])

    forward_step(0)
    for p in range(PIECES):
        relay(0, c, p, False).wait_recv()
    acc[...] = dot_nn(ns[c * 2], wall[c * 2]) + dot_nn(ns[c * 2 + 1], wall[c * 2 + 1])
    for t in range(C - 1):
        if t + 1 < C - 1:
            forward_step(t + 1)
        use_step(t)

    for i in range(1, N):
        peer = (me + i) % N
        remote(ns.at[peer], nall.at[me], nsem.at[0], nsem.at[1], peer).start()

    row_pos = lax.broadcasted_iota(jnp.int32, (L, L), 0)
    col_pos = lax.broadcasted_iota(jnp.int32, (L, L), 1)
    causal = (row_pos >= col_pos)[None]

    def attend(k, carry):
        rows = pl.ds(pl.multiple_of(k * L, L), L)
        for j in range(KH):
            kp = acc[rows, j * HEAD_DIM:(j + 1) * HEAD_DIM]
            key = (kp * cos + pltpu.roll(kp, HEAD_DIM // 2, 1) * sin).astype(BF16)
            key_s[k, j] = key
            val_s[k, j] = acc[rows, KV + j * HEAD_DIM:KV + (j + 1) * HEAD_DIM].astype(BF16)
            sc = dot_nt(qst[k, j], key) * scale
            raised = jnp.where(causal, jnp.exp(sc.reshape(G, L, L)), 0.0)
            pr = raised / jnp.sum(raised, axis=-1, keepdims=True)
            prob[k, j] = pr.reshape(G * L, L)
        return carry
    lax.fori_loop(0, B, attend, 0)

    def usend(k, j):
        return pltpu.make_async_remote_copy(
            src_ref=lowb.at[k, j], dst_ref=ubuf.at[k, j], send_sem=us.at[k, j],
            recv_sem=ur.at[k, j], device_id=(lax.max(sec - 1, 0), me), device_id_type=MESH)

    def kbcopy(k, j, i):
        peer = ((c + i) % C) * 2 + core
        ref = kball.at[me, k, j]
        return remote(ref, ref, kbs.at[k, i], kbr.at[k, i], peer)

    def kbpartner(k, j):
        ref = kball.at[me, k, j]
        return remote(ref, ref, kbs.at[k, 0], kbr.at[k, 0], partner)

    def kbrelay(k, i, mine):
        chip = (c - i + C) % C
        ref = kball.at[chip * 2 + (core if mine else 1 - core), k]
        return remote(ref, ref, krs.at[k, i], krr.at[k, i], partner)

    def turn(k, carry):
        rows = pl.ds(pl.multiple_of(k * L, L), L)
        keys, values = [], []
        for j in range(KH):
            @pl.when(sec == S - 1)
            def _(j=j):
                cot_copy(k, j).wait()

            @pl.when(sec < S - 1)
            def _(j=j):
                usend(k, j).wait_recv()
            u = ubuf[k, j]
            us_ = jnp.concatenate(
                [u[:, g * HEAD_DIM:(g + 1) * HEAD_DIM] for g in range(G)], axis=0)
            key, q, pr = key_s[k, j], qst[k, j], prob[k, j]
            gp = dot_nt(us_, val_s[k, j])
            gv = dot_tn(pr.astype(BF16), us_).astype(BF16)
            rd = jnp.sum(pr * gp, axis=-1, keepdims=True)
            gs = (pr * (gp - rd) * scale).astype(BF16)
            gk = dot_tn(gs, q)
            gk = (gk * cos - pltpu.roll(gk, HEAD_DIM // 2, 1) * sin).astype(BF16)
            keys.append(gk)
            values.append(gv)
            kball[me, k, j] = jnp.concatenate([gk, gv], axis=1)
            gq = dot_nn(gs, key)
            for g in range(G):
                v = gq[g * L:(g + 1) * L]
                col = (j * G + g) * HEAD_DIM
                gnb[col // w, :, col % w:col % w + HEAD_DIM] = (
                    v * cos - pltpu.roll(v, HEAD_DIM // 2, 1) * sin)
            kbpartner(k, j).start()
            for i in range(1, C):
                kbcopy(k, j, i).start()
        kbv = jnp.concatenate(keys + values, axis=1)
        part_inv = inv_s[rows, 0:1]
        proj = jnp.zeros((L, 1), F32)
        for d in range(N):
            gn = gnb[d] + dot_nt(kbv, wall[d])
            gnb[d] = gn
            gt = gn * x_ref[rows, d * w:(d + 1) * w].astype(F32) * part_inv
            proj = proj + jnp.sum(gt * gall[d][0:1, :], axis=-1, keepdims=True)
            gsh[d] += jnp.sum(gt.reshape(L // 8, 8, w), axis=0)
        proj = proj * (1.0 / D) * part_inv * part_inv
        for j in range(KH):
            for e in range(N // KH):
                d = j * (N // KH) + e
                u = ubuf[k, j, :, e * w:(e + 1) * w].astype(F32)
                xd = x_ref[rows, d * w:(d + 1) * w].astype(F32)
                low = (u + part_inv * gall[d][0:1, :] * gnb[d] - xd * proj).astype(BF16)
                lowb[k, j, :, e * w:(e + 1) * w] = low
                low_out[rows, d * w:(d + 1) * w] = low

            @pl.when(sec > 0)
            def _(j=j):
                usend(k, j).start()
        return carry
    lax.fori_loop(0, B, turn, 0)

    gsall[me] = gsh[me]
    for i in range(1, N):
        peer = (me + i) % N
        remote(gsh.at[peer], gsall.at[me], ssem.at[0], ssem.at[1], peer).start()
    for k in range(B):
        for i in range(1, C):
            chip = (c - i + C) % C
            wait_all(kball.at[chip * 2 + core, k], kbr.at[k, i])
            kbrelay(k, i, True).start()
    wait_all(nall.at[pl.ds(0, N - 1)], nsem.at[1])
    for k in range(B):
        wait_all(kball.at[partner, k], kbr.at[k, 0])
        for i in range(1, C):
            kbrelay(k, i, False).wait_recv()
    rows_all = nall[...].reshape(N * B * L, w)
    for j in range(KH):
        back = jnp.concatenate(
            [kball[g, k, j] for g in range(N) for k in range(B)], axis=0)
        dw = dot_tn(rows_all, back)
        gk_out[:, j * HEAD_DIM:(j + 1) * HEAD_DIM] = dw[:, :HEAD_DIM]
        gv_out[:, j * HEAD_DIM:(j + 1) * HEAD_DIM] = dw[:, HEAD_DIM:]
    wait_all(gsall.at[pl.ds(0, N - 1)], ssem.at[1])
    gg = gsall[0]
    for d in range(1, N):
        gg = gg + gsall[d]
    gg_out[...] = jnp.broadcast_to(jnp.sum(gg, axis=0, keepdims=True), gg_out.shape)

    wait_all(gall.at[pl.ds(0, N - 1)], gsem.at[0])
    wait_all(nall.at[pl.ds(0, N - 1)], nsem.at[0])
    wait_all(gsall.at[pl.ds(0, N - 1)], ssem.at[0])
    for p in range(PIECES):
        relay(0, c, p, True).wait_send()
        for way in range(2):
            for t in range(C - 1):
                @pl.when(can_send(way, t))
                def _(way=way, t=t, p=p):
                    wcopy(way, t, p).wait_send()

                @pl.when(can_recv(way, t))
                def _(way=way, t=t, p=p):
                    chip = c - 1 - t if way == 0 else c + 1 + t
                    relay(1 + way * (C - 1) + t, chip, p, True).wait_send()
    for k in range(B):
        for i in range(C):
            wait_all(kball.at[me, k], kbs.at[k, i])
            if i:
                kbrelay(k, i, True).wait_send()

    @pl.when(sec > 0)
    def _():
        for k in range(B):
            for j in range(KH):
                usend(k, j).wait_send()


def body(S, N, inputs, cotangent, norm_gain, key_weight, value_weight, plan):
    B, L, D = inputs.shape[1:]
    w, KV = key_weight.shape[1:]
    KH = KV // HEAD_DIM
    CW = D // KH
    G = CW // HEAD_DIM
    C = N // 2
    cos, sin = rope_tables(L)
    gain8 = jnp.broadcast_to(norm_gain.astype(F32), (8, w))
    vmem = pl.BlockSpec(memory_space=pltpu.VMEM)
    hbm = pl.BlockSpec(memory_space=pl.ANY)
    dma = pltpu.SemaphoreType.DMA
    low, gk, gv, gg = pl.pallas_call(
        functools.partial(kernel, S, N),
        out_shape=(
            jax.ShapeDtypeStruct((B * L, D), BF16),
            jax.ShapeDtypeStruct((w, KV), F32),
            jax.ShapeDtypeStruct((w, KV), F32),
            jax.ShapeDtypeStruct((8, w), F32),
        ),
        in_specs=[vmem, hbm, vmem, hbm, hbm, vmem, vmem],
        out_specs=(vmem,) * 4,
        scratch_shapes=[
            pltpu.VMEM((N, w, 2 * KV), BF16),
            pltpu.VMEM((N, B * L, w), BF16),
            pltpu.VMEM((N, B * L, w), BF16),
            pltpu.VMEM((N, 8, w), F32),
            pltpu.VMEM((B * L, 128), F32),
            pltpu.VMEM((B * L, 2 * KV), F32),
            pltpu.VMEM((B, KH, L, HEAD_DIM), BF16),
            pltpu.VMEM((B, KH, L, HEAD_DIM), BF16),
            pltpu.VMEM((B, KH, G * L, HEAD_DIM), BF16),
            pltpu.VMEM((B, KH, G * L, L), F32),
            pltpu.VMEM((B, KH, L, CW), BF16),
            pltpu.VMEM((B, KH, L, CW), BF16),
            pltpu.VMEM((N, L, w), F32),
            pltpu.VMEM((N, B, KH, L, 2 * HEAD_DIM), BF16),
            pltpu.VMEM((N, 8, w), F32),
            pltpu.VMEM((N, 8, w), F32),
            dma((2,)),
            dma((2, C - 1, PIECES)),
            dma((2, C - 1, PIECES)),
            dma((2 * C - 1, PIECES)),
            dma((2 * C - 1, PIECES)),
            dma((2,)),
            dma((2,)),
            dma((2,)),
            dma((B, KH)),
            dma((B, KH)),
            dma((B, KH)),
            dma((B, C)),
            dma((B, C)),
            dma((B, C)),
            dma((B, C)),
        ],
        compiler_params=pltpu.CompilerParams(
            collective_id=0, has_side_effects=True, vmem_limit_bytes=56 * 1024 * 1024),
    )(inputs[0].reshape(B * L, D), cotangent, gain8, key_weight[0], value_weight[0],
      jnp.asarray(cos), jnp.asarray(sin))
    low = low.reshape(B, L, D)
    selector = plan[0][:, None] == jnp.arange(B, dtype=jnp.int32)[None, :]
    ordered = jnp.sum(
        jnp.where(selector[:, :, None, None], low[None], jnp.zeros((), BF16)), axis=1)
    return ordered[None], gk[None], gv[None], gg[0:1]


def solution(mesh):
    in_specs = (
        P("section", None, "dp", None),
        P(None, "dp", None),
        P("section", "dp"),
        P("section", "dp", None),
        P("section", "dp", None),
        P("section", None),
    )
    out_specs = (
        P("section", None, "dp", None),
        P("section", "dp", None),
        P("section", "dp", None),
        P("section", "dp"),
    )
    run = functools.partial(body, mesh.shape["section"], mesh.shape["dp"])
    return jax.shard_map(run, mesh=mesh, in_specs=in_specs, out_specs=out_specs, check_vma=False)
```

time: 430 us -> 177 us (0.41)
  waiting for transfers between devices: 271 us -> 0 us
  Pallas kernels: 0 us -> 167 us
  matrix products: 51.9 us -> 0 us
  blocking collectives: 29.5 us -> 0 us
  local copies, waits for them, and re-layouts: 29.3 us -> 4.48 us
  other arithmetic: 24.8 us -> 4.5 us
  between operations: 14.6 us -> 0.65 us
  starting transfers between devices: 6.56 us -> 0 us
    pallas_call x0 -> x1, Pallas kernels: none -> 167 us  [body(): pl.pallas_call(functools.partial(kernel, S, N), out_shape=(jax.ShapeDtype...]
    ppermute x5 -> x0, waiting for transfers between devices: 143 us -> none  [from_behind(): lax.ppermute(value, axis, [(source, source + steps) for source in range(f...]
    reduce_scatter x2 -> x0, waiting for transfers between devices: 70.3 us -> none  [the longest x1 47.8 us: body(): lax.psum_scatter(sum_key.astype(jnp.bfloat16), 'dp', scatter_dimension=0,...]
    all_gather x2 -> x0, waiting for transfers between devices: 56.2 us -> none  [the longest x1 29 us: body(): lax.all_gather(value_weight[0], 'dp', axis=0, tiled=True)]
    dot_general x16 -> x0, matrix products: 48.3 us -> none  [the longest x4 16 us: contract_cols(): lax.dot_general(left, right, (((1,), (1,)), ((), ())), preferred_element_...]
    unnamed x1 -> x0, blocking collectives: 14.9 us -> none
    all_gather x1 -> x0, blocking collectives: 14.6 us -> none  [body(): lax.all_gather(norm_gain[0], 'dp', axis=0, tiled=True)]
    dot_general x1 -> x0, local copies, waits for them, and re-layouts: 6.48 us -> none  [body(): key_pre = jnp.dot(normed, full_key, preferred_element_type=jnp.float32)]
  transfers between devices with their start and end apart: 9 -> 0, of which waited for: 9 -> 0; matrix products, arithmetic and copies ran while one was open for 8% -> 0% of each run, Pallas kernels for 0% -> 0%
where the time goes in v1:
time: 177 us; the launch traced here: 176 us
  Pallas kernels  167 us (94%)
  other arithmetic  4.5 us (3%)
  local copies, waits for them, and re-layouts  4.48 us (3%)
    pallas_call x1, Pallas kernels, body(): pl.pallas_call(functools.partial(kernel, S, N), out_shape=(jax.ShapeDtype...  167 us

profile of v1, /device:TPU:0, one launch (start us, length us, event | category | flops | bytes accessed | tf_op | source)
XLA Modules:
  0.0 176.4 jit_solution(9792513171906569747)
XLA Ops:
  0.6 0.7 iota_compare_fusion
  1.4 0.7 broadcast_in_dim.53
  2.0 0.6 broadcast_in_dim.46.gain_ref
  2.7 166.8 %shard_map.111 = (bf16[128,4096]{1,0:T(8,128)(2,1)}, f32[512,512]{1,0:T(8,128)}, f32[512,512]{1,0:T(8,128)}, f32[8,512]{1,0:T(8,128)}) custom-call(bf16[128,4096]{1,0:T(8,128)(2,1)} %bitcast.9, bf16[2,64,4096]{2,1,0:T(8,128)(2,1)} %cot_ref.1, f32[8,512]{1,0:T(8,128)} %broadcast_in_dim.46.gain_ref, bf16[512,512]{1,0:T(8,128)(2,1)} %bitcast.14, ...), custom_call_target="tpu_custom_call" | custom-call | tf_op jit(solution)/shard_map/pallas_call | solution.py:366
  169.5 0.0 copy-start.1
  169.5 3.1 %select_reduce_fusion = bf16[2,64,4096]{2,1,0:T(8,128)(2,1)} fusion(pred[2,2]{1,0:T(4,128)(4,1)S(1)} %iota_compare_fusion, bf16[2,64,4096]{2,1,0:T(8,128)(2,1)} %bitcast.11), kind=kLoop, calls=%fused_computation | loop fusion | flops 1572864 | bytes 2097156 | tf_op jit(solution)/shard_map/reduce_sum | solution.py:415
  172.6 1.3 slice.3
  173.9 0.0 copy-done.1
  173.9 0.0 copy-start
  173.9 1.0 copy.14
  174.8 0.6 copy-done
  175.5 1.0 copy.15
Async XLA Ops:
  169.5 4.4 %copy-start.1 = (f32[512,512]{1,0:T(8,128)S(1)}, f32[512,512]{1,0:T(8,128)}, u32[]{:S(2)}) copy-start(f32[512,512]{1,0:T(8,128)} %get-tuple-element.9) | copy-start | bytes 3145732
  173.9 1.6 copy-start

commit v2 on v1

--- a/solution.py
+++ b/solution.py
@@ -12,7 +12,8 @@
 HEAD_DIM = 128
 EPS = 1e-05
 ROPE_BASE = 500000.0
-PIECES = 2
+PIECES = 4
+HELPED = 1
 MESH = pl.DeviceIdType.MESH
 F32 = jnp.float32
 BF16 = jnp.bfloat16
@@ -44,8 +45,8 @@
 def kernel(S, N, x_ref, cot_ref, gain_ref, wk_ref, wv_ref, cos_ref, sin_ref,
            low_out, gk_out, gv_out, gg_out,
            wall, ns, nall, gall, inv_s, acc, key_s, val_s, qst, prob, ubuf, lowb, gnb,
-           kball, gsh, gsall,
-           loc, ws, wr, rls, rlr, gsem, nsem, ssem, us, ur, uloc, kbs, kbr, krs, krr):
+           kball, gsh, gsall, stage,
+           loc, ws, wr, hs, hr, ps, pr_sem, token, rls, rlr, gsem, nsem, ssem, us, ur, uloc, kbs, kbr, krs, krr):
     B, KH, L = ubuf.shape[0], ubuf.shape[1], ubuf.shape[2]
     CW = ubuf.shape[3]
     w = wall.shape[1]
@@ -60,6 +61,9 @@
     core = me % 2
     partner = c * 2 + (1 - core)
     hp = w // PIECES
+    OWN = PIECES - HELPED if S % 2 == 0 else PIECES
+    upper = sec >= S // 2
+    pair = jnp.where(upper, sec - S // 2, sec + S // 2) if S % 2 == 0 else sec
 
     def remote(src, dst, send, recv, peer):
         return pltpu.make_async_remote_copy(
@@ -85,9 +89,12 @@
     @pl.when(sec < S - 1)
     def _():
         pl.semaphore_signal(barrier, inc=1, device_id=(sec + 1, me), device_id_type=MESH)
+    helps = S % 2 == 0 and S > 2
+    if helps:
+        pl.semaphore_signal(barrier, inc=1, device_id=(pair, me), device_id_type=MESH)
     below = jnp.where(sec > 0, 1, 0)
     above = jnp.where(sec < S - 1, 1, 0)
-    pl.semaphore_wait(barrier, N - 1 + below + above)
+    pl.semaphore_wait(barrier, N - 1 + below + above + (1 if helps else 0))
 
     gcopies = []
     for i in range(1, N):
@@ -114,7 +121,32 @@
 
     def relay(slot, chip, p, mine):
         ref = piece(chip * 2 + (core if mine else 1 - core), p)
-        return remote(ref, ref, rls.at[slot, p], rlr.at[slot, p], partner)
+        return remote(ref, ref, rls.at[slot], rlr.at[slot], partner)
+
+    def relayed(slot, chip, mine, sem):
+        wait_all(wall.at[chip * 2 + (core if mine else 1 - core)], sem.at[slot])
+
+    def to_pair(p):
+        return pltpu.make_async_remote_copy(
+            src_ref=piece(me, p), dst_ref=stage.at[c, p - OWN], send_sem=ps.at[0, p - OWN],
+            recv_sem=pr_sem.at[0, p - OWN], device_id=(pair, me), device_id_type=MESH)
+
+    def hcopy(way, t, p, receive=False):
+        if receive:
+            chip, peer = (c - 1 - t if way == 0 else c + 1 + t), partner
+        else:
+            chip = c - t if way == 0 else c + t
+            peer = (c + 1 if way == 0 else c - 1) * 2 + core
+        ref = stage.at[chip, p - OWN]
+        return remote(ref, ref, hs.at[way, t, p - OWN], hr.at[way, t, p - OWN], peer)
+
+    def hand(way, t, p):
+        chip = c - 1 - t if way == 0 else c + 1 + t
+        slot = 1 + way * (C - 1) + t
+        return pltpu.make_async_remote_copy(
+            src_ref=stage.at[chip, p - OWN], dst_ref=piece(chip * 2 + core, p),
+            send_sem=ps.at[slot, p - OWN], recv_sem=pr_sem.at[slot, p - OWN],
+            device_id=(pair, me), device_id_type=MESH)
 
     def can_send(way, t):
         return ((c - t >= 0) & (c + 1 < C)) if way == 0 else ((c + t < C) & (c >= 1))
@@ -122,11 +154,16 @@
     def can_recv(way, t):
         return (c - 1 - t >= 0) if way == 0 else (c + 1 + t < C)
 
-    for p in range(PIECES):
+    for p in range(OWN, PIECES):
+        @pl.when(upper)
+        def _(p=p):
+            to_pair(p).start()
+    for p in range(OWN):
         for way in range(2):
-            @pl.when(can_send(way, 0))
+            @pl.when(can_send(way, 0) & upper)
             def _(way=way, p=p):
                 wcopy(way, 0, p).start()
+    for p in range(PIECES):
         relay(0, c, p, True).start()
 
     def cot_copy(k, j):
@@ -168,14 +205,26 @@
     def forward_step(t):
         for p in range(PIECES):
             for way in range(2):
+                chip = c - 1 - t if way == 0 else c + 1 + t
+
                 @pl.when(can_recv(way, t))
-                def _(way=way, p=p):
-                    wrecv(way, t, p).wait_recv()
-                    if t + 1 < C - 1:
-                        @pl.when(can_send(way, t + 1))
+                def _(way=way, p=p, chip=chip):
+                    def by_line():
+                        wrecv(way, t, p).wait_recv()
+                        if t + 1 < C - 1:
+                            @pl.when(can_send(way, t + 1))
+                            def _():
+                                wcopy(way, t + 1, p).start()
+                    if p < OWN:
+                        by_line()
+                    else:
+                        @pl.when(upper)
                         def _():
-                            wcopy(way, t + 1, p).start()
-                    chip = c - 1 - t if way == 0 else c + 1 + t
+                            hand(way, t, p).wait_recv()
+
+                        @pl.when(jnp.logical_not(upper))
+                        def _():
+                            by_line()
                     relay(1 + way * (C - 1) + t, chip, p, True).start()
 
     def use_step(t):
@@ -183,14 +232,41 @@
             @pl.when(can_recv(way, t))
             def _(way=way):
                 chip = c - 1 - t if way == 0 else c + 1 + t
-                for p in range(PIECES):
-                    relay(1 + way * (C - 1) + t, chip, p, False).wait_recv()
+                relayed(1 + way * (C - 1) + t, chip, False, rlr)
                 acc[...] += dot_nn(ns[chip * 2], wall[chip * 2]) + dot_nn(
                     ns[chip * 2 + 1], wall[chip * 2 + 1])
 
+    @pl.when(jnp.logical_not(upper))
+    def _():
+        for t in range(C - 1):
+            for p in range(OWN, PIECES):
+                if t == 0:
+                    to_pair(p).wait_recv()
+                for way in range(2):
+                    if t == 0:
+                        @pl.when(can_send(way, 0))
+                        def _(way=way, p=p):
+                            hcopy(way, 0, p).start()
+            for p in range(OWN, PIECES):
+                for way in range(2):
+                    if t + 1 == C - 1:
+                        for q in range(PIECES) if p == OWN else ():
+                            @pl.when(can_send(way, 0))
+                            def _(way=way, q=q):
+                                wcopy(way, 0, q).start()
+            for p in range(OWN, PIECES):
+                for way in range(2):
+                    @pl.when(can_recv(way, t))
+                    def _(way=way, p=p, t=t):
+                        hcopy(way, t, p, True).wait_recv()
+                        if t + 1 < C - 1:
+                            @pl.when(can_send(way, t + 1))
+                            def _():
+                                hcopy(way, t + 1, p).start()
+                        hand(way, t, p).start()
+
     forward_step(0)
-    for p in range(PIECES):
-        relay(0, c, p, False).wait_recv()
+    relayed(0, c, False, rlr)
     acc[...] = dot_nn(ns[c * 2], wall[c * 2]) + dot_nn(ns[c * 2 + 1], wall[c * 2 + 1])
     for t in range(C - 1):
         if t + 1 < C - 1:
@@ -237,6 +313,12 @@
         chip = (c - i + C) % C
         ref = kball.at[chip * 2 + (core if mine else 1 - core), k]
         return remote(ref, ref, krs.at[k, i], krr.at[k, i], partner)
+
+    def sent(k):
+        @pl.when(sec > 0)
+        def _():
+            for j in range(KH):
+                usend(k, j).wait_send()
 
     def turn(k, carry):
         rows = pl.ds(pl.multiple_of(k * L, L), L)
@@ -271,6 +353,10 @@
             kbpartner(k, j).start()
             for i in range(1, C):
                 kbcopy(k, j, i).start()
+        @pl.when((sec == S - 1) & (k > 0))
+        def _():
+            sent(k - 1)
+            pl.semaphore_signal(token, inc=1, device_id=(sec, partner), device_id_type=MESH)
         kbv = jnp.concatenate(keys + values, axis=1)
         part_inv = inv_s[rows, 0:1]
         proj = jnp.zeros((L, 1), F32)
@@ -281,6 +367,9 @@
             proj = proj + jnp.sum(gt * gall[d][0:1, :], axis=-1, keepdims=True)
             gsh[d] += jnp.sum(gt.reshape(L // 8, 8, w), axis=0)
         proj = proj * (1.0 / D) * part_inv * part_inv
+        @pl.when((sec == S - 1) & ((k > 0) | (core > 0)))
+        def _():
+            pl.semaphore_wait(token, 1)
         for j in range(KH):
             for e in range(N // KH):
                 d = j * (N // KH) + e
@@ -295,6 +384,11 @@
                 usend(k, j).start()
         return carry
     lax.fori_loop(0, B, turn, 0)
+
+    @pl.when((sec == S - 1) & (core == 0))
+    def _():
+        sent(B - 1)
+        pl.semaphore_signal(token, inc=1, device_id=(sec, partner), device_id_type=MESH)
 
     gsall[me] = gsh[me]
     for i in range(1, N):
@@ -326,29 +420,44 @@
     wait_all(gall.at[pl.ds(0, N - 1)], gsem.at[0])
     wait_all(nall.at[pl.ds(0, N - 1)], nsem.at[0])
     wait_all(gsall.at[pl.ds(0, N - 1)], ssem.at[0])
-    for p in range(PIECES):
-        relay(0, c, p, True).wait_send()
-        for way in range(2):
-            for t in range(C - 1):
-                @pl.when(can_send(way, t))
+    relayed(0, c, True, rls)
+    for way in range(2):
+        for t in range(C - 1):
+            for p in range(PIECES):
+                @pl.when(can_send(way, t) if p < OWN else can_send(way, t) & jnp.logical_not(upper))
                 def _(way=way, t=t, p=p):
                     wcopy(way, t, p).wait_send()
 
-                @pl.when(can_recv(way, t))
+            @pl.when(can_recv(way, t))
+            def _(way=way, t=t):
+                chip = c - 1 - t if way == 0 else c + 1 + t
+                relayed(1 + way * (C - 1) + t, chip, True, rls)
+            for p in range(OWN, PIECES):
+                @pl.when(can_send(way, t) & jnp.logical_not(upper))
                 def _(way=way, t=t, p=p):
-                    chip = c - 1 - t if way == 0 else c + 1 + t
-                    relay(1 + way * (C - 1) + t, chip, p, True).wait_send()
+                    hcopy(way, t, p).wait_send()
+
+                @pl.when(can_recv(way, t) & jnp.logical_not(upper))
+                def _(way=way, t=t, p=p):
+                    hand(way, t, p).wait_send()
+    for p in range(OWN, PIECES):
+        @pl.when(upper)
+        def _(p=p):
+            to_pair(p).wait_send()
     for k in range(B):
         for i in range(C):
             wait_all(kball.at[me, k], kbs.at[k, i])
             if i:
                 kbrelay(k, i, True).wait_send()
 
-    @pl.when(sec > 0)
+    @pl.when(sec < S - 1)
     def _():
         for k in range(B):
-            for j in range(KH):
-                usend(k, j).wait_send()
+            sent(k)
+
+    @pl.when((sec == S - 1) & (core == 1))
+    def _():
+        sent(B - 1)
 
 
 def body(S, N, inputs, cotangent, norm_gain, key_weight, value_weight, plan):
@@ -390,11 +499,17 @@
             pltpu.VMEM((N, B, KH, L, 2 * HEAD_DIM), BF16),
             pltpu.VMEM((N, 8, w), F32),
             pltpu.VMEM((N, 8, w), F32),
+            pltpu.VMEM((C, HELPED, w // PIECES, 2 * KV), BF16),
             dma((2,)),
             dma((2, C - 1, PIECES)),
             dma((2, C - 1, PIECES)),
-            dma((2 * C - 1, PIECES)),
-            dma((2 * C - 1, PIECES)),
+            dma((2, C - 1, HELPED)),
+            dma((2, C - 1, HELPED)),
+            dma((2 * C - 1, HELPED)),
+            dma((2 * C - 1, HELPED)),
+            pltpu.SemaphoreType.REGULAR,
+            dma((2 * C - 1,)),
+            dma((2 * C - 1,)),
             dma((2,)),
             dma((2,)),
             dma((2,)),

time: 177 us -> 169 us (0.955)
  Pallas kernels: 167 us -> 159 us
    pallas_call x1, Pallas kernels: 167 us -> 159 us  [body(): pl.pallas_call(functools.partial(kernel, S, N), out_shape=(jax.ShapeDtype...]
where the time goes in v2:
time: 169 us
  Pallas kernels  159 us (94%)
  other arithmetic  4.5 us (3%)
  local copies, waits for them, and re-layouts  4.48 us (3%)
    pallas_call x1, Pallas kernels, body(): pl.pallas_call(functools.partial(kernel, S, N), out_shape=(jax.ShapeDtype...  159 us

profile of v2, /device:TPU:0, one launch (start us, length us, event | category | flops | bytes accessed | tf_op | source)
XLA Modules:
  0.0 168.6 jit_solution(15741450384642078050)
XLA Ops:
  0.6 0.7 iota_compare_fusion
  1.4 0.7 broadcast_in_dim.53
  2.0 0.6 broadcast_in_dim.46.gain_ref
  2.7 159.0 %shard_map.111 = (bf16[128,4096]{1,0:T(8,128)(2,1)}, f32[512,512]{1,0:T(8,128)}, f32[512,512]{1,0:T(8,128)}, f32[8,512]{1,0:T(8,128)}) custom-call(bf16[128,4096]{1,0:T(8,128)(2,1)} %bitcast.9, bf16[2,64,4096]{2,1,0:T(8,128)(2,1)} %cot_ref.1, f32[8,512]{1,0:T(8,128)} %broadcast_in_dim.46.gain_ref, bf16[512,512]{1,0:T(8,128)(2,1)} %bitcast.14, ...), custom_call_target="tpu_custom_call" | custom-call | tf_op jit(solution)/shard_map/pallas_call | solution.py:475
  161.6 0.0 copy-start.1
  161.6 3.1 %select_reduce_fusion = bf16[2,64,4096]{2,1,0:T(8,128)(2,1)} fusion(pred[2,2]{1,0:T(4,128)(4,1)S(1)} %iota_compare_fusion, bf16[2,64,4096]{2,1,0:T(8,128)(2,1)} %bitcast.11), kind=kLoop, calls=%fused_computation | loop fusion | flops 1572864 | bytes 2097156 | tf_op jit(solution)/shard_map/reduce_sum | solution.py:530
  164.7 1.3 slice.3
  166.0 0.0 copy-done.1
  166.0 0.0 copy-start
  166.0 1.0 copy.14
  167.0 0.6 copy-done
  167.6 1.0 copy.15
Async XLA Ops:
  161.6 4.4 %copy-start.1 = (f32[512,512]{1,0:T(8,128)S(1)}, f32[512,512]{1,0:T(8,128)}, u32[]{:S(2)}) copy-start(f32[512,512]{1,0:T(8,128)} %get-tuple-element.9) | copy-start | bytes 3145732
  166.0 1.6 copy-start

commit v3 on v2

--- a/solution.py
+++ b/solution.py
@@ -249,8 +249,11 @@
                             hcopy(way, 0, p).start()
             for p in range(OWN, PIECES):
                 for way in range(2):
-                    if t + 1 == C - 1:
-                        for q in range(PIECES) if p == OWN else ():
+                    if p == OWN:
+                        for q in range(PIECES):
+                            if q != t and not (t + 1 == C - 1 and q > t):
+                                continue
+
                             @pl.when(can_send(way, 0))
                             def _(way=way, q=q):
                                 wcopy(way, 0, q).start()

time: 169 us -> 166 us (0.982)
  Pallas kernels: 159 us -> 156 us
    pallas_call x1, Pallas kernels: 159 us -> 156 us  [body(): pl.pallas_call(functools.partial(kernel, S, N), out_shape=(jax.ShapeDtype...]
where the time goes in v3:
time: 166 us; the launch traced here: 165 us
  Pallas kernels  156 us (94%)
  other arithmetic  4.5 us (3%)
  local copies, waits for them, and re-layouts  4.48 us (3%)
    pallas_call x1, Pallas kernels, body(): pl.pallas_call(functools.partial(kernel, S, N), out_shape=(jax.ShapeDtype...  156 us

profile of v3, /device:TPU:0, one launch (start us, length us, event | category | flops | bytes accessed | tf_op | source)
XLA Modules:
  0.0 165.3 jit_solution(5953152827979368675)
XLA Ops:
  0.6 0.7 iota_compare_fusion
  1.4 0.7 broadcast_in_dim.53
  2.0 0.6 broadcast_in_dim.46.gain_ref
  2.7 155.7 %shard_map.111 = (bf16[128,4096]{1,0:T(8,128)(2,1)}, f32[512,512]{1,0:T(8,128)}, f32[512,512]{1,0:T(8,128)}, f32[8,512]{1,0:T(8,128)}) custom-call(bf16[128,4096]{1,0:T(8,128)(2,1)} %bitcast.9, bf16[2,64,4096]{2,1,0:T(8,128)(2,1)} %cot_ref.1, f32[8,512]{1,0:T(8,128)} %broadcast_in_dim.46.gain_ref, bf16[512,512]{1,0:T(8,128)(2,1)} %bitcast.14, ...), custom_call_target="tpu_custom_call" | custom-call | tf_op jit(solution)/shard_map/pallas_call | solution.py:478
  158.3 0.0 copy-start.1
  158.3 3.1 %select_reduce_fusion = bf16[2,64,4096]{2,1,0:T(8,128)(2,1)} fusion(pred[2,2]{1,0:T(4,128)(4,1)S(1)} %iota_compare_fusion, bf16[2,64,4096]{2,1,0:T(8,128)(2,1)} %bitcast.11), kind=kLoop, calls=%fused_computation | loop fusion | flops 1572864 | bytes 2097156 | tf_op jit(solution)/shard_map/reduce_sum | solution.py:533
  161.4 1.3 slice.3
  162.7 0.0 copy-done.1
  162.7 0.0 copy-start
  162.7 1.0 copy.14
  163.7 0.6 copy-done
  164.3 1.0 copy.15
Async XLA Ops:
  158.3 4.4 %copy-start.1 = (f32[512,512]{1,0:T(8,128)S(1)}, f32[512,512]{1,0:T(8,128)}, u32[]{:S(2)}) copy-start(f32[512,512]{1,0:T(8,128)} %get-tuple-element.9) | copy-start | bytes 3145732
  162.7 1.6 copy-start
